TPU v7x, 256 devices: a whole 4x4x8 slice. The times are simulated.
256 devices in a mesh: section: 2 (over x_hi), feat: 16 (over y, x_lo, core), width: 8 (over z).
Axes of the slice: x: 4 (x_hi: 2, x_lo: 2; x = x_hi * 2 + x_lo), y: 4, z: 8, core: 2. Of those that a mesh axis runs over, the one named last changes fastest.
Arguments:
- mlp_inputs: bfloat16 [4, 1024, 2304], P('section', 'width'), may hold values from -6 to 6
- encoder: bfloat16 [4, 2304, 16384], P('section', 'width', 'feat'), may hold values from -0.125 to 0.125
- enc_bias: float32 [4, 16384], P('section', 'feat'), may hold values from -3 to 3
- decoder: bfloat16 [10, 16384, 2304], P('section', 'feat', 'width'), may hold values from -0.046875 to 0.046875
- dec_bias: float32 [4, 2304], P(None, 'width'), may hold values from -3 to 3
- targets: bfloat16 [4, 1024, 2304], P(None, None, 'width'), may hold values from -6 to 6
- live_rows: int32 [1024], replicated, may hold values 0 or 1
Outputs:
- errors: bfloat16 [4, 1024, 2304], P(None, None, 'width')
- gradients: bfloat16 [10, 16384, 2304], P('section', 'feat', 'width')
All inputs are finite; a program needn't handle non-finite values.
Results may differ from a plain program's by a relative error of at most 0.0042.
Values may be sent and summed in bfloat16 or wider, within the bound.
No kernel may reach another device: no remote copies, remote signals or barrier semaphores. Data moves between devices by JAX's collectives and lax.ppermute only.
A program may use at most 128 MiB of HBM per device.

v0:
```python
import jax
import jax.numpy as jnp
from jax import lax
from jax.sharding import PartitionSpec as P


def from_behind(value, axis, steps):
    count = lax.axis_size(axis)
    initial, last = (max(0, -steps), min(count, count - steps))
    return lax.ppermute(value, axis, [(source, source + steps) for source in range(initial, last)])


def pair_tables(layer_count):
    source_ids = []
    target_ids = []
    for source in range(layer_count):
        for target in range(source, layer_count):
            source_ids.append(source)
            target_ids.append(target)
    return (jnp.array(source_ids, jnp.int32), jnp.array(target_ids, jnp.int32))


def local(mlp_inputs, encoder, enc_bias, decoder, dec_bias, targets, live_rows):
    layers_here, tok_local, model_width = mlp_inputs.shape
    pre_act = jnp.einsum(
        "ltd,ldf->tlf",
        mlp_inputs,
        lax.all_gather(encoder, "width", axis=1, tiled=True),
        preferred_element_type=jnp.float32,
    )
    local_feats = jnp.maximum(pre_act + enc_bias[None, :, :], 0.0).astype(jnp.bfloat16)
    token_feats = lax.all_gather(local_feats, "width", axis=0, tiled=True)
    layers_all = dec_bias.shape[0]
    tokens_all = live_rows.shape[0]
    per_section = decoder.shape[0]
    source_ids, target_ids = pair_tables(layers_all)
    section_id = lax.axis_index("section")
    earlier = from_behind(token_feats[:, layers_here - 1], "section", 1)
    features = jnp.concatenate([earlier[:, None, :], token_feats], axis=1)
    first_layer = section_id * layers_here - 1
    rebuilt = jnp.zeros((layers_all, tokens_all, decoder.shape[2]), jnp.float32)
    chosen = []
    for pair_slot in range(per_section):
        pair_id = section_id * per_section + pair_slot
        source = source_ids[pair_id]
        target = target_ids[pair_id]
        picked = lax.dynamic_index_in_dim(features, source - first_layer, 1, keepdims=False)
        chosen.append((picked, target))
        partial_value = jnp.dot(picked, decoder[pair_slot], preferred_element_type=jnp.float32)
        current = lax.dynamic_index_in_dim(rebuilt, target, 0, keepdims=False)
        rebuilt = lax.dynamic_update_index_in_dim(rebuilt, current + partial_value, target, 0)
    summed = lax.psum(rebuilt, ("section", "feat"))
    keep_rows = live_rows.astype(jnp.float32)[None, :, None]
    errors = ((summed + dec_bias[:, None, :] - targets.astype(jnp.float32)) * keep_rows).astype(
        jnp.bfloat16
    )
    gradients = []
    for picked, target in chosen:
        residual = lax.dynamic_index_in_dim(errors, target, 0, keepdims=False)
        product = lax.dot_general(
            picked, residual, (((0,), (0,)), ((), ())), preferred_element_type=jnp.float32
        )
        gradients.append((product / tokens_all).astype(jnp.bfloat16))
    return (errors, jnp.stack(gradients))


def solution(mesh):
    placed = (
        P("section", "width", None),
        P("section", "width", "feat"),
        P("section", "feat"),
        P("section", "feat", "width"),
        P(None, "width"),
        P(None, None, "width"),
        P(),
    )
    return jax.shard_map(
        local,
        mesh=mesh,
        in_specs=placed,
        out_specs=(P(None, None, "width"), P("section", "feat", "width")),
        check_vma=False,
    )
```

profile of v0, /device:TPU:1, one launch (start us, length us, event | category | flops | bytes accessed | tf_op | source)
XLA Modules:
  0.0 397.8 jit_solution(8431505922366384273)
XLA Ops:
  7.2 0.0 all-gather.3.cloned.1.call-start
  7.2 0.7 all-gather.3.cloned.1.call-update
  7.9 0.0 all-gather.5.cloned.1.call-start
  8.0 109.4 %all-gather.3.cloned.1.call-done = bf16[2,2304,1024]{2,1,0:T(8,128)(2,1)} async-done(((bf16[2,288,1024]{2,1,0:T(8,128)(2,1)}), bf16[2,2304,1024]{2,1,0:T(8,128)(2,1)}) %all-gather.3.cloned.1.call-update) | async-done | bytes 9437200 | tf_op jit(solution)/shard_map/all_gather | solution.py:28
  117.3 7.3 %fusion.36 = bf16[128,2,1024]{0,2,1:T(8,128)(2,1)} fusion(bf16[2,2304,1024]{2,1,0:T(8,128)(2,1)} %all-gather.3.cloned.1.call-done, bf16[2,128,2304]{2,1,0:T(8,128)(2,1)S(1)} %copy-done, f32[2,1024]{1,0:T(2,128)} %param.11), kind=kOutput, calls=%fused_computation.59 | convolution fusion | flops 1208745984 | bytes 11149312 | tf_op jit(solution)/shard_map/ltd,ldf->tlf/dot_general | solution.py:25
  124.7 0.0 all-reduce.2.cloned.1.call-start
  124.7 57.6 %all-gather.5.cloned.1.call-done = bf16[1024,2,1024]{0,2,1:T(8,128)(2,1)} async-done(((bf16[128,2,1024]{0,2,1:T(8,128)(2,1)}), bf16[1024,2,1024]{0,2,1:T(8,128)(2,1)}) %all-gather.5.cloned.1.call-update) | async-done | bytes 4194320 | tf_op jit(solution)/shard_map/all_gather | solution.py:32
  182.4 3.1 slice_bitcast_fusion
  185.4 4.4 %collective-permute-start = (bf16[1024,1024]{0,1:T(8,128)(2,1)}, bf16[1024,1024]{0,1:T(8,128)(2,1)S(1)}, u32[]{:S(2)}, u32[]{:S(2)}) collective-permute-start(bf16[1024,1024]{0,1:T(8,128)(2,1)} %slice_bitcast_fusion), channel_id=1, source_target_pairs={{0,128},{1,129},{2,130},{3,131},{4,132},{5,133},{6,134},{7,135},{8... | collective-permute-start | bytes 6291464 | tf_op jit(solution)/shard_map/ppermute | solution.py:10
  189.9 0.7 fusion.72
  203.2 26.7 %collective-permute-done = bf16[1024,1024]{0,1:T(8,128)(2,1)S(1)} collective-permute-done((bf16[1024,1024]{0,1:T(8,128)(2,1)}, bf16[1024,1024]{0,1:T(8,128)(2,1)S(1)}, u32[]{:S(2)}, u32[]{:S(2)}) %collective-permute-start) | collective-permute-done | bytes 2097184 | tf_op jit(solution)/shard_map/ppermute | solution.py:10
  229.9 3.0 broadcast_in_dim.25
  232.9 0.8 copy-done.1
  233.7 3.4 fusion.18
  237.1 1.3 constant_dynamic-slice_fusion.3
  238.5 2.2 fusion.17
  240.7 1.3 constant_dynamic-slice_fusion.2
  242.1 2.2 fusion.15
  244.3 1.3 constant_dynamic-slice_fusion.1
  245.6 2.3 fusion.13
  247.9 1.3 constant_dynamic-slice_fusion
  249.3 2.2 fusion.11
  251.5 0.7 copy-done.8
  252.2 126.4 %all-reduce.2.cloned.1.call-done = f32[4,1024,288]{1,2,0:T(8,128)} async-done(((f32[4,1024,288]{1,2,0:T(8,128)}), f32[4,1024,288]{1,2,0:T(8,128)}) %all-reduce.2.cloned.1.call-update) | async-done | bytes 4718608 | tf_op jit(solution)/shard_map/psum | solution.py:52
  378.6 3.9 multiply_convert_fusion
  382.5 0.3 copy-done.2
  382.8 1.4 fusion.35
  384.2 1.4 fusion.33
  385.6 1.4 fusion.31
  386.9 1.4 fusion.29
  388.3 1.4 fusion.27
  389.7 1.6 copy-done.9
  (19 shorter events, 0.1 us)
Async XLA Ops:
  7.2 110.2 %copy-start = (bf16[2,128,2304]{2,1,0:T(8,128)(2,1)S(1)}, bf16[2,128,2304]{2,1,0:T(8,128)(2,1)}, u32[]{:S(2)}) copy-start(bf16[2,128,2304]{2,1,0:T(8,128)(2,1)} %param.9) | copy-start | bytes 3538948
  7.2 110.2 %all-gather.3.cloned.1.call-start = ((), (), s32[]{:S(2)}) async-start(), calls=%async_computation | async-start | bytes 10616832 | tf_op jit(solution)/shard_map/all_gather | solution.py:28
  7.9 174.4 %all-gather.5.cloned.1.call-start = ((), (), s32[]{:S(2)}) async-start(), calls=%async_computation.1 | async-start | bytes 4718592 | tf_op jit(solution)/shard_map/all_gather | solution.py:32
  124.7 65.2 %copy-start.5 = (s32[10]{0:T(128)S(1)}, s32[10]{0:T(128)}, u32[]{:S(2)}) copy-start(s32[10]{0:T(128)} %constant.92.clone) | copy-start | bytes 124
  124.7 65.2 %copy-start.6 = (s32[10]{0:T(128)S(1)}, s32[10]{0:T(128)}, u32[]{:S(2)}) copy-start(s32[10]{0:T(128)} %constant.93.clone) | copy-start | bytes 124
  124.7 253.9 %all-reduce.2.cloned.1.call-start = ((), (), s32[]{:S(2)}) async-start(), calls=%async_computation.2 | async-start | bytes 9437184 | tf_op jit(solution)/shard_map/psum | solution.py:52
  185.4 44.5 %collective-permute-start = (bf16[1024,1024]{0,1:T(8,128)(2,1)}, bf16[1024,1024]{0,1:T(8,128)(2,1)S(1)}, u32[]{:S(2)}, u32[]{:S(2)}) collective-permute-start(bf16[1024,1024]{0,1:T(8,128)(2,1)} %slice_bitcast_fusion), channel_id=1, source_target_pairs={{0,128},{1,129},{2,130},{3,131},{4,132},{5,133},{6,134},{7,135},{8... | collective-permute-start | bytes 6291464 | tf_op jit(solution)/shard_map/ppermute | solution.py:10
  229.9 3.8 copy-start.1
  233.7 4.7 %copy-start.3 = (bf16[5,1024,288]{1,2,0:T(8,128)(2,1)S(1)}, bf16[5,1024,288]{1,2,0:T(8,128)(2,1)}, u32[]{:S(2)}) copy-start(bf16[5,1024,288]{1,2,0:T(8,128)(2,1)} %param.12) | copy-start | bytes 8847364
  251.5 0.7 copy-start.8
  251.5 127.1 %copy-start.7 = (f32[4,288]{1,0:T(4,128)S(1)}, f32[4,288]{1,0:T(4,128)}, u32[]{:S(2)}) copy-start(f32[4,288]{1,0:T(4,128)} %param.13) | copy-start | bytes 13828
  378.6 4.2 %copy-start.2 = (bf16[1024,2,1024]{0,2,1:T(8,128)(2,1)S(1)}, bf16[1024,2,1024]{0,2,1:T(8,128)(2,1)}, u32[]{:S(2)}) copy-start(bf16[1024,2,1024]{0,2,1:T(8,128)(2,1)} %all-gather.5.cloned.1.call-done) | copy-start | bytes 12582916
  382.8 5.5 %copy-start.4 = (bf16[4,1024,288]{1,2,0:T(8,128)(2,1)}, bf16[4,1024,288]{1,2,0:T(8,128)(2,1)S(1)}, u32[]{:S(2)}) copy-start(bf16[4,1024,288]{1,2,0:T(8,128)(2,1)S(1)} %multiply_convert_fusion) | copy-start | bytes 7077892
  389.7 1.6 copy-start.9
Sparse Core Ops, SparseCore 0:
  9.8 107.5 all-gather.2
  124.8 57.5 all-gather.4
  251.6 126.9 all-reduce.1
where the time goes:
time: 398 us
  waiting for transfers between devices  321 us (81%)
  matrix products  26.5 us (7%)
  between operations  26.5 us (7%)
  local copies, waits for them, and re-layouts  15.5 us (4%)
  starting transfers between devices  4.52 us (1%)
    psum x1, waiting for transfers between devices, local(): summed = lax.psum(rebuilt, ('section', 'feat'))  126 us
    all_gather x1, waiting for transfers between devices, local(): lax.all_gather(encoder, 'width', axis=1, tiled=True)  109 us
    all_gather x1, waiting for transfers between devices, local(): token_feats = lax.all_gather(local_feats, 'width', axis=0, tiled=True)  57.6 us
    ppermute x1, waiting for transfers between devices, from_behind(): lax.ppermute(value, axis, [(source, source + steps) for source in range(i...  26.7 us
    dot_general x5, matrix products, local(): jnp.dot(picked, decoder[pair_slot], preferred_element_type=jnp.float32)  12.3 us
  transfers between devices with their start and end apart: 4, of which 4 were waited for; matrix products, arithmetic and copies ran while one was open for 0% of the time, Pallas kernels for 0%

commit v1 on v0

--- a/solution.py
+++ b/solution.py
@@ -49,7 +49,7 @@
         partial_value = jnp.dot(picked, decoder[pair_slot], preferred_element_type=jnp.float32)
         current = lax.dynamic_index_in_dim(rebuilt, target, 0, keepdims=False)
         rebuilt = lax.dynamic_update_index_in_dim(rebuilt, current + partial_value, target, 0)
-    summed = lax.psum(rebuilt, ("section", "feat"))
+    summed = lax.psum(lax.psum(rebuilt, "feat"), "section")
     keep_rows = live_rows.astype(jnp.float32)[None, :, None]
     errors = ((summed + dec_bias[:, None, :] - targets.astype(jnp.float32)) * keep_rows).astype(
         jnp.bfloat16

time: 398 us -> 554 us (1.39)
  waiting for transfers between devices: 321 us -> 477 us
    psum x1 -> x2, waiting for transfers between devices: 126 us -> 282 us  [local(): summed = lax.psum(lax.psum(rebuilt, 'feat'), 'section')]
  transfers between devices with their start and end apart: 4 -> 5, of which waited for: 4 -> 5; matrix products, arithmetic and copies ran while one was open for 0% -> 0% of each run, Pallas kernels for 0% -> 0%
where the time goes in v1:
time: 554 us
  waiting for transfers between devices  477 us (86%)
  matrix products  26.5 us (5%)
  between operations  26.5 us (5%)
  local copies, waits for them, and re-layouts  15.5 us (3%)
    psum x2, waiting for transfers between devices, local(): summed = lax.psum(lax.psum(rebuilt, 'feat'), 'section')  282 us
    all_gather x1, waiting for transfers between devices, local(): lax.all_gather(encoder, 'width', axis=1, tiled=True)  109 us
    all_gather x1, waiting for transfers between devices, local(): token_feats = lax.all_gather(local_feats, 'width', axis=0, tiled=True)  57.6 us
    ppermute x1, waiting for transfers between devices, from_behind(): lax.ppermute(value, axis, [(source, source + steps) for source in range(i...  26.9 us
    dot_general x5, matrix products, local(): jnp.dot(picked, decoder[pair_slot], preferred_element_type=jnp.float32)  12.3 us
  transfers between devices with their start and end apart: 5, of which 5 were waited for; matrix products, arithmetic and copies ran while one was open for 0% of the time, Pallas kernels for 0%

profile of v1, /device:TPU:1, one launch (start us, length us, event | category | flops | bytes accessed | tf_op | source)
XLA Modules:
  0.0 553.9 jit_solution(1117009901755562962)
XLA Ops:
  7.2 0.7 all-gather.3.cloned.1.call-update
  8.0 109.4 %all-gather.3.cloned.1.call-done = bf16[2,2304,1024]{2,1,0:T(8,128)(2,1)} async-done(((bf16[2,288,1024]{2,1,0:T(8,128)(2,1)}), bf16[2,2304,1024]{2,1,0:T(8,128)(2,1)}) %all-gather.3.cloned.1.call-update) | async-done | bytes 9437200 | tf_op jit(solution)/shard_map/all_gather | solution.py:28
  117.3 7.3 %fusion.36 = bf16[128,2,1024]{0,2,1:T(8,128)(2,1)} fusion(bf16[2,2304,1024]{2,1,0:T(8,128)(2,1)} %all-gather.3.cloned.1.call-done, bf16[2,128,2304]{2,1,0:T(8,128)(2,1)S(1)} %copy-done, f32[2,1024]{1,0:T(2,128)} %param.11), kind=kOutput, calls=%fused_computation.59 | convolution fusion | flops 1208745984 | bytes 11149312 | tf_op jit(solution)/shard_map/ltd,ldf->tlf/dot_general | solution.py:25
  124.7 0.0 all-reduce.3.cloned.1.call-start
  124.7 57.6 %all-gather.5.cloned.1.call-done = bf16[1024,2,1024]{0,2,1:T(8,128)(2,1)} async-done(((bf16[128,2,1024]{0,2,1:T(8,128)(2,1)}), bf16[1024,2,1024]{0,2,1:T(8,128)(2,1)}) %all-gather.5.cloned.1.call-update) | async-done | bytes 4194320 | tf_op jit(solution)/shard_map/all_gather | solution.py:32
  182.4 3.1 slice_bitcast_fusion
  185.4 4.2 collective-permute-start
  189.7 0.7 fusion.72
  203.0 26.9 %collective-permute-done = bf16[1024,1024]{0,1:T(8,128)(2,1)S(1)} collective-permute-done((bf16[1024,1024]{0,1:T(8,128)(2,1)}, bf16[1024,1024]{0,1:T(8,128)(2,1)S(1)}, u32[]{:S(2)}, u32[]{:S(2)}) %collective-permute-start) | collective-permute-done | bytes 2097184 | tf_op jit(solution)/shard_map/ppermute | solution.py:10
  229.9 3.0 broadcast_in_dim.25
  232.9 0.8 copy-done.1
  233.7 3.4 fusion.18
  237.1 1.3 constant_dynamic-slice_fusion.3
  238.5 2.2 fusion.17
  240.7 1.3 constant_dynamic-slice_fusion.2
  242.1 2.2 fusion.15
  244.3 1.3 constant_dynamic-slice_fusion.1
  245.6 2.3 fusion.13
  247.9 1.3 constant_dynamic-slice_fusion
  249.3 2.2 fusion.11
  251.5 0.2 all-reduce.5.cloned.1.call-start
  251.7 146.7 %all-reduce.3.cloned.1.call-done = f32[4,1024,288]{1,2,0:T(8,128)} async-done(((f32[4,1024,288]{1,2,0:T(8,128)}), f32[4,1024,288]{1,2,0:T(8,128)}) %all-reduce.3.cloned.1.call-update) | async-done | bytes 4718608 | tf_op jit(solution)/shard_map/psum | solution.py:52
  398.5 0.7 copy-done.8
  399.1 135.5 %all-reduce.5.cloned.1.call-done = f32[4,1024,288]{1,2,0:T(8,128)} async-done(((f32[4,1024,288]{1,2,0:T(8,128)}), f32[4,1024,288]{1,2,0:T(8,128)}) %all-reduce.5.cloned.1.call-update) | async-done | bytes 4718608 | tf_op jit(solution)/shard_map/psum | solution.py:52
  534.6 3.9 multiply_convert_fusion
  538.6 0.3 copy-done.2
  538.9 1.4 fusion.35
  540.2 1.4 fusion.33
  541.6 1.4 fusion.31
  543.0 1.4 fusion.29
  544.4 1.4 fusion.27
  545.8 1.6 copy-done.9
  (22 shorter events, 0.2 us)
Async XLA Ops:
  7.2 110.2 %copy-start = (bf16[2,128,2304]{2,1,0:T(8,128)(2,1)S(1)}, bf16[2,128,2304]{2,1,0:T(8,128)(2,1)}, u32[]{:S(2)}) copy-start(bf16[2,128,2304]{2,1,0:T(8,128)(2,1)} %param.9) | copy-start | bytes 3538948
  7.2 110.2 %all-gather.3.cloned.1.call-start = ((), (), s32[]{:S(2)}) async-start(), calls=%async_computation | async-start | bytes 10616832 | tf_op jit(solution)/shard_map/all_gather | solution.py:28
  7.9 174.4 %all-gather.5.cloned.1.call-start = ((), (), s32[]{:S(2)}) async-start(), calls=%async_computation.1 | async-start | bytes 4718592 | tf_op jit(solution)/shard_map/all_gather | solution.py:32
  124.7 65.0 %copy-start.5 = (s32[10]{0:T(128)S(1)}, s32[10]{0:T(128)}, u32[]{:S(2)}) copy-start(s32[10]{0:T(128)} %constant.92.clone) | copy-start | bytes 124
  124.7 65.0 %copy-start.6 = (s32[10]{0:T(128)S(1)}, s32[10]{0:T(128)}, u32[]{:S(2)}) copy-start(s32[10]{0:T(128)} %constant.93.clone) | copy-start | bytes 124
  124.7 273.8 %all-reduce.3.cloned.1.call-start = ((), (), s32[]{:S(2)}) async-start(), calls=%async_computation.2 | async-start | bytes 9437184 | tf_op jit(solution)/shard_map/psum | solution.py:52
  185.4 44.5 %collective-permute-start = (bf16[1024,1024]{0,1:T(8,128)(2,1)}, bf16[1024,1024]{0,1:T(8,128)(2,1)S(1)}, u32[]{:S(2)}, u32[]{:S(2)}) collective-permute-start(bf16[1024,1024]{0,1:T(8,128)(2,1)} %slice_bitcast_fusion), channel_id=1, source_target_pairs={{0,128},{1,129},{2,130},{3,131},{4,132},{5,133},{6,134},{7,135},{8... | collective-permute-start | bytes 6291464 | tf_op jit(solution)/shard_map/ppermute | solution.py:10
  229.9 3.8 copy-start.1
  233.7 4.7 copy-start.3
  251.5 283.1 %all-reduce.5.cloned.1.call-start = ((), (), s32[]{:S(2)}) async-start(), calls=%async_computation.3 | async-start | bytes 9437184 | tf_op jit(solution)/shard_map/psum | solution.py:52
  398.4 0.7 copy-start.8
  398.4 136.2 %copy-start.7 = (f32[4,288]{1,0:T(4,128)S(1)}, f32[4,288]{1,0:T(4,128)}, u32[]{:S(2)}) copy-start(f32[4,288]{1,0:T(4,128)} %param.13) | copy-start | bytes 13828
  534.6 4.2 copy-start.2
  538.9 5.5 copy-start.4
  545.8 1.6 copy-start.9
Sparse Core Ops, SparseCore 0:
  9.8 107.5 all-gather.2
  124.8 57.5 all-gather.4
  251.6 146.7 all-reduce.2
  401.0 133.5 all-reduce.4
